TPU v7x, 256 devices: a whole 4x4x8 slice. The times are simulated.
256 devices in a mesh: row: 32 (over y, x, core), col: 8 (over z).
Axes of the slice: x: 4, y: 4, z: 8, core: 2. Of those that a mesh axis runs over, the one named last changes fastest.
Arguments:
- vectors_window: float32 [32, 32, 64, 1024], P(None, 'row', None, 'col'), may hold values from -6 to 6
- column_strip: float32 [32, 32, 64, 1024], P(None, 'row', None, 'col'), may hold values from -6 to 6
- row_strip: float32 [1024, 64, 8, 128], P('row', None, 'col'), may hold values from -6 to 6
- factor: float32 [1024, 1024], P('row', 'col'), may hold values from -2 to 2
- window_start: int32 [1], replicated, may hold values from 1 to 64512
- deflated: int32 [1], replicated, may hold values from 0 to 512
Outputs:
- vectors_updated: float32 [32, 32, 64, 1024], P(None, 'row', None, 'col')
- column_updated: float32 [32, 32, 64, 1024], P(None, 'row', None, 'col')
- row_updated: float32 [1024, 64, 8, 128], P('row', None, 'col')
All inputs are finite; a program needn't handle non-finite values.
Results may differ from a plain program's by a relative error of at most 0.0003.
Values sent between devices are 32-bit elements; how exact they have to be, the bound alone decides.
A program may use at most 64 MiB of HBM per device.

v0:
```python
import jax
import jax.numpy as jnp
from jax import lax
from jax.sharding import PartitionSpec as P

W = 1024


def from_everyone(x, axis):
    peers = lax.axis_size(axis)
    return lax.all_to_all(jnp.broadcast_to(x[None], (peers, *x.shape)), axis, 0, 0, tiled=True)


def laid_out(pieces, dim):
    dims = list(pieces.shape[1:])
    dims[dim] *= pieces.shape[0]
    return jnp.moveaxis(pieces, 0, dim).reshape(dims)


def gather_directly(x, axis, dim):
    pieces = from_everyone(x, axis)
    return laid_out(pieces, dim)


def reflect(factor, deflated):
    columns = jnp.arange(W, dtype=jnp.int32)
    kept_count = W - deflated[0]
    spike_row = jnp.where(columns < kept_count, factor[0], 0.0)
    squares = jnp.sum(spike_row * spike_row)
    corner = factor[0, 0]
    magnitude = jnp.sqrt(squares + 1e-06)
    signum = jnp.where(corner >= 0, 1.0, -1.0)
    vector = spike_row + jnp.where(columns == 0, signum * magnitude, 0.0)
    denominator = squares + 2.0 * jnp.abs(corner) * magnitude + magnitude * magnitude
    scaling = 2.0 / denominator
    reflected_image = jnp.dot(factor, vector, precision=lax.Precision.HIGHEST)
    return factor - scaling * reflected_image[:, None] * vector[None, :]


def body(vectors_window, column_strip, row_strip, factor, window_start, deflated):
    highest = lax.Precision.HIGHEST
    row_position = lax.axis_index("row")
    column_position = lax.axis_index("col")
    start_row = window_start[0]
    widened = gather_directly(factor, "col", 1)
    rotation = reflect(lax.all_gather(widened, "row", axis=0, tiled=True), deflated)
    rounds = vectors_window.shape[0]
    blocks = vectors_window.shape[2]
    local_width = vectors_window.shape[3]
    z_blocks = vectors_window.reshape(rounds, blocks, local_width)
    strip_blocks = column_strip.reshape(rounds, blocks, local_width)
    z_turned = jnp.einsum(
        "rbk,kj->rbj",
        lax.all_to_all(z_blocks, "col", split_axis=1, concat_axis=2, tiled=True),
        rotation,
        precision=highest,
    )
    strip_turned = jnp.einsum(
        "rbk,kj->rbj",
        lax.all_to_all(strip_blocks, "col", split_axis=1, concat_axis=2, tiled=True),
        rotation,
        precision=highest,
    )
    z_rotated = lax.all_to_all(z_turned, "col", split_axis=2, concat_axis=1, tiled=True)
    strip_rotated = lax.all_to_all(strip_turned, "col", split_axis=2, concat_axis=1, tiled=True)
    row_count = lax.axis_size("row")
    round_number = jnp.arange(rounds, dtype=jnp.int32)[:, None]
    block_number = jnp.arange(blocks, dtype=jnp.int32)[None, :]
    row_number = (round_number * row_count + row_position) * blocks + block_number
    column_updated = jnp.where(
        row_number[:, :, None] < start_row, strip_rotated, strip_blocks
    ).reshape(column_strip.shape)
    vectors_updated = z_rotated.reshape(vectors_window.shape)
    strip_rows = row_strip.shape[0]
    flat_strip = row_strip.reshape(strip_rows, -1)
    stacked = lax.all_to_all(flat_strip, "row", split_axis=1, concat_axis=0, tiled=True)
    rotated_rows = lax.dot_general(rotation, stacked, (((0,), (0,)), ((), ())), precision=highest)
    returned = lax.all_to_all(rotated_rows, "row", split_axis=0, concat_axis=1, tiled=True)
    column_count = lax.axis_size("col")
    column_rounds = row_strip.shape[1]
    column_block = row_strip.shape[3]
    round_index = jnp.arange(column_rounds, dtype=jnp.int32)[:, None]
    lane_index = jnp.arange(column_block, dtype=jnp.int32)[None, :]
    column_number = (round_index * column_count + column_position) * column_block + lane_index
    row_updated = jnp.where(
        column_number[None, :, None, :] >= start_row + W,
        returned.reshape(row_strip.shape),
        row_strip,
    )
    return (vectors_updated, column_updated, row_updated)


def solution(mesh):
    return jax.shard_map(
        body,
        mesh=mesh,
        in_specs=(
            P(None, "row", None, "col"),
            P(None, "row", None, "col"),
            P("row", None, "col", None),
            P("row", "col"),
            P(),
            P(),
        ),
        out_specs=(
            P(None, "row", None, "col"),
            P(None, "row", None, "col"),
            P("row", None, "col", None),
        ),
        check_vma=False,
    )
```

profile of v0, /device:TPU:1, one launch (start us, length us, event | category | flops | bytes accessed | tf_op | source)
XLA Modules:
  0.0 231.8 jit_solution(5835078651876137352)
XLA Ops:
  7.9 16.6 %all_to_all.106 = f32[8,32,128]{2,1,0:T(8,128)S(1)} all-to-all(f32[8,32,128]{2,1,0:T(8,128)S(1)} %broadcast_in_dim.44), channel_id=1, replica_groups=mesh['row'=32,'col'=8] {'col'}, dimensions={0} | all-to-all | bytes 262144 | tf_op jit(solution)/shard_map/all_to_all | solution.py:11
  25.7 4.4 %reduce.3 = f32[32,64,128]{2,1,0:T(8,128)S(1)} reduce(f32[32,64,1,128]{3,2,1,0:T(1,128)} %param.8, f32[]{:T(128)} %broadcast.101), dimensions={2}, to_apply=%param.8.reduce_sub_computation.3 | reduce | bytes 2097156 | tf_op args[2]
  32.0 9.4 %all-to-all-start.5 = ((f32[32,32,256]{2,0,1:T(8,128)}), f32[32,32,256]{2,0,1:T(8,128)S(1)}, u32[]{:S(2)}, u32[]{:S(2)}) async-start(f32[32,32,256]{2,0,1:T(8,128)} %copy.61), calls=%async_computation.5 | async-start | bytes 2097152 | tf_op jit(solution)/shard_map/all_to_all | solution.py:76
  44.2 14.1 %all-to-all-done.5 = f32[32,32,256]{2,0,1:T(8,128)S(1)} async-done(((f32[32,32,256]{2,0,1:T(8,128)}), f32[32,32,256]{2,0,1:T(8,128)S(1)}, u32[]{:S(2)}, u32[]{:S(2)}) %all-to-all-start.5) | async-done | bytes 1048608 | tf_op jit(solution)/shard_map/all_to_all | solution.py:76
  58.4 3.6 %all-to-all-start.1 = ((f32[32,64,128]{2,0,1:T(8,128)}), f32[32,64,128]{2,0,1:T(8,128)S(1)}, u32[]{:S(2)}, u32[]{:S(2)}) async-start(f32[32,64,128]{2,0,1:T(8,128)} %bitcast.78), calls=%async_computation.1 | async-start | bytes 2097152 | tf_op jit(solution)/shard_map/all_to_all | solution.py:54
  64.2 16.0 %all-gather.2.cloned.1.call-done = f32[1024,1024]{1,0:T(8,128)} async-done(((f32[32,1024]{1,0:T(8,128)}), f32[1024,1024]{1,0:T(8,128)}) %all-gather.2.cloned.1.call-update) | async-done | bytes 4194320 | tf_op jit(solution)/shard_map/all_gather | solution.py:46
  81.0 10.2 %all-to-all-done.1 = f32[32,64,128]{2,0,1:T(8,128)S(1)} async-done(((f32[32,64,128]{2,0,1:T(8,128)}), f32[32,64,128]{2,0,1:T(8,128)S(1)}, u32[]{:S(2)}, u32[]{:S(2)}) %all-to-all-start.1) | async-done | bytes 1048608 | tf_op jit(solution)/shard_map/all_to_all | solution.py:54
  91.2 3.7 %all-to-all-start.3 = ((f32[32,64,128]{2,0,1:T(8,128)}), f32[32,64,128]{2,0,1:T(8,128)S(1)}, u32[]{:S(2)}, u32[]{:S(2)}) async-start(f32[32,64,128]{2,0,1:T(8,128)} %bitcast.76), calls=%async_computation.3 | async-start | bytes 2097152 | tf_op jit(solution)/shard_map/all_to_all | solution.py:60
  99.4 5.8 %fusion.17 = f32[1,1024]{1,0:T(1,128)S(1)} fusion(f32[1024,1]{0,1:T(1,128)S(1)} %bitcast.101, f32[1024,1024]{1,0:T(8,128)} %all-gather.2.cloned.1.call-done), kind=kOutput, calls=%fused_computation.32 | convolution fusion | flops 12582912 | bytes 4202496 | tf_op jit(solution)/shard_map/dot_general | solution.py:36
  107.6 5.4 %copy.60 = f32[1024,1024]{1,0:T(8,128)} copy(f32[1024,1024]{0,1:T(8,128)} %fusion.4) | data formatting | bytes 8388608 | tf_op jit(solution)/shard_map/dot_general | solution.py:77
  113.0 6.6 %fusion.18 = f32[32,32,256]{2,1,0:T(8,128)} fusion(f32[32,32,1024]{2,1,0:T(8,128)} %bitcast.85, f32[1024,256,1]{1,0,2:T(8,128)S(1)} %bitcast.92), kind=kOutput, calls=%fused_computation.33 | convolution fusion | flops 3221225472 | bytes 6291456 | tf_op jit(solution)/shard_map/dot_general | solution.py:77
  121.9 5.0 %all-to-all-start.6 = ((f32[32,32,256]{2,1,0:T(8,128)}), f32[32,32,256]{2,1,0:T(8,128)S(1)}, u32[]{:S(2)}, u32[]{:S(2)}) async-start(f32[32,32,256]{2,1,0:T(8,128)} %fusion.18), calls=%async_computation.6 | async-start | bytes 2097152 | tf_op jit(solution)/shard_map/all_to_all | solution.py:78
  130.8 6.4 %fusion.9 = f32[32,8,1024]{2,0,1:T(8,128)S(1)} fusion(f32[32,8,1024]{2,0,1:T(8,128)} %all_to_all.81, f32[1024,1024]{1,0:T(8,128)} %all-gather.2.cloned.1.call-done, f32[1024]{0:T(1024)S(1)} %bitcast.98, f32[1024]{0:T(1024)S(1)} %broadcast_multiply_fusion), kind=kOutput, calls=%fused_computation.10 | convolution fusion | flops 3223322624 | bytes 6299648 | tf_op jit(solution)/shard_map/rbk,kj->rbj/dot_general | solution.py:52
  140.0 4.8 %reshape.143 = f32[8,1,32768]{2,1,0:T(1,128)} reshape(f32[1024,8,32]{2,1,0:T(8,128)} %bitcast.81) | data formatting | bytes 2097152
  145.8 4.3 %all-to-all-start.2 = ((f32[8,1,32768]{2,1,0:T(1,128)}), f32[8,1,32768]{2,1,0:T(1,128)S(1)}, u32[]{:S(2)}, u32[]{:S(2)}) async-start(f32[8,1,32768]{2,1,0:T(1,128)} %reshape.143), calls=%async_computation.2 | async-start | bytes 2097152 | tf_op jit(solution)/shard_map/all_to_all | solution.py:64
  151.8 6.4 %fusion.12 = f32[32,8,1024]{2,0,1:T(8,128)S(1)} fusion(f32[32,8,1024]{2,0,1:T(8,128)} %all_to_all.88, f32[1024,1024]{1,0:T(8,128)} %all-gather.2.cloned.1.call-done, f32[1024]{0:T(1024)S(1)} %bitcast.99, f32[1024]{0:T(1024)S(1)} %broadcast_multiply_fusion), kind=kOutput, calls=%fused_computation.11 | convolution fusion | flops 3223322624 | bytes 6299648 | tf_op jit(solution)/shard_map/rbk,kj->rbj/dot_general | solution.py:58
  160.9 4.9 %reshape.145 = f32[8,1,32768]{2,1,0:T(1,128)} reshape(f32[1024,8,32]{2,1,0:T(8,128)} %bitcast.82) | data formatting | bytes 2097152
  165.9 13.5 %all-to-all-done.2 = f32[8,1,32768]{2,1,0:T(1,128)S(1)} async-done(((f32[8,1,32768]{2,1,0:T(1,128)}), f32[8,1,32768]{2,1,0:T(1,128)S(1)}, u32[]{:S(2)}, u32[]{:S(2)}) %all-to-all-start.2) | async-done | bytes 1048608 | tf_op jit(solution)/shard_map/all_to_all | solution.py:64
  179.3 4.2 %all-to-all-start.4 = ((f32[8,1,32768]{2,1,0:T(1,128)}), f32[8,1,32768]{2,1,0:T(1,128)}, u32[]{:S(2)}, u32[]{:S(2)}) async-start(f32[8,1,32768]{2,1,0:T(1,128)} %reshape.145), calls=%async_computation.4 | async-start | bytes 2097152 | tf_op jit(solution)/shard_map/all_to_all | solution.py:65
  192.0 3.3 %reshape.144 = f32[1024,8,32]{2,1,0:T(8,128)} reshape(f32[8,32768]{1,0:T(8,128)S(1)} %reduce.4) | data formatting | bytes 2097152
  195.3 3.9 %copy.55 = f32[32,8,8,128]{3,2,1,0:T(8,128)} copy(f32[32,8,8,128]{0,2,3,1:T(8,128)} %bitcast.83) | data formatting | bytes 2097152 | tf_op jit(solution)/shard_map/all_to_all | solution.py:64
  199.3 13.5 %all-to-all-done.4 = f32[8,1,32768]{2,1,0:T(1,128)} async-done(((f32[8,1,32768]{2,1,0:T(1,128)}), f32[8,1,32768]{2,1,0:T(1,128)}, u32[]{:S(2)}, u32[]{:S(2)}) %all-to-all-start.4) | async-done | bytes 1048608 | tf_op jit(solution)/shard_map/all_to_all | solution.py:65
  212.8 4.3 %reduce.5 = f32[8,32768]{1,0:T(8,128)S(1)} reduce(f32[8,1,32768]{2,1,0:T(1,128)} %all-to-all-done.4, f32[]{:T(128)} %broadcast.102), dimensions={1}, to_apply=%all_to_all.89.reduce_sub_computation | reduce | bytes 2097156 | tf_op jit(solution)/shard_map/all_to_all | solution.py:65
  217.1 3.3 %reshape.146 = f32[1024,8,32]{2,1,0:T(8,128)} reshape(f32[8,32768]{1,0:T(8,128)S(1)} %reduce.5) | data formatting | bytes 2097152
  (47 shorter events, 39.8 us)
Async XLA Ops:
  7.2 73.1 %all-gather.2.cloned.1.call-start = ((), (), s32[]{:S(2)}) async-start(), calls=%async_computation.7 | async-start | bytes 4325376 | tf_op jit(solution)/shard_map/all_gather | solution.py:46
  30.5 32.2 %copy-start.2 = (f32[32,1,64,128]{3,2,1,0:T(8,128)S(1)}, f32[32,1,64,128]{3,2,1,0:T(8,128)}, u32[]{:S(2)}) copy-start(f32[32,1,64,128]{3,2,1,0:T(8,128)} %param.7) | copy-start | bytes 3145732
  32.0 26.3 %all-to-all-start.5 = ((f32[32,32,256]{2,0,1:T(8,128)}), f32[32,32,256]{2,0,1:T(8,128)S(1)}, u32[]{:S(2)}, u32[]{:S(2)}) async-start(f32[32,32,256]{2,0,1:T(8,128)} %copy.61), calls=%async_computation.5 | async-start | bytes 2097152 | tf_op jit(solution)/shard_map/all_to_all | solution.py:76
  58.4 32.8 %all-to-all-start.1 = ((f32[32,64,128]{2,0,1:T(8,128)}), f32[32,64,128]{2,0,1:T(8,128)S(1)}, u32[]{:S(2)}, u32[]{:S(2)}) async-start(f32[32,64,128]{2,0,1:T(8,128)} %bitcast.78), calls=%async_computation.1 | async-start | bytes 2097152 | tf_op jit(solution)/shard_map/all_to_all | solution.py:54
  91.2 30.7 %all-to-all-start.3 = ((f32[32,64,128]{2,0,1:T(8,128)}), f32[32,64,128]{2,0,1:T(8,128)S(1)}, u32[]{:S(2)}, u32[]{:S(2)}) async-start(f32[32,64,128]{2,0,1:T(8,128)} %bitcast.76), calls=%async_computation.3 | async-start | bytes 2097152 | tf_op jit(solution)/shard_map/all_to_all | solution.py:60
  99.4 5.8 %copy-start = (f32[1024,1024]{1,0:T(8,128)S(1)}, f32[1024,1024]{1,0:T(8,128)}, u32[]{:S(2)}) copy-start(f32[1024,1024]{1,0:T(8,128)} %all-gather.2.cloned.1.call-done) | copy-start | bytes 12582916
  121.9 22.9 %all-to-all-start.6 = ((f32[32,32,256]{2,1,0:T(8,128)}), f32[32,32,256]{2,1,0:T(8,128)S(1)}, u32[]{:S(2)}, u32[]{:S(2)}) async-start(f32[32,32,256]{2,1,0:T(8,128)} %fusion.18), calls=%async_computation.6 | async-start | bytes 2097152 | tf_op jit(solution)/shard_map/all_to_all | solution.py:78
  144.8 1.0 copy-start.4
  145.8 33.6 %all-to-all-start.2 = ((f32[8,1,32768]{2,1,0:T(1,128)}), f32[8,1,32768]{2,1,0:T(1,128)S(1)}, u32[]{:S(2)}, u32[]{:S(2)}) async-start(f32[8,1,32768]{2,1,0:T(1,128)} %reshape.143), calls=%async_computation.2 | async-start | bytes 2097152 | tf_op jit(solution)/shard_map/all_to_all | solution.py:64
  160.9 23.5 %copy-start.5 = (f32[32,32,256]{2,1,0:T(8,128)S(1)}, f32[32,32,256]{2,1,0:T(8,128)}, u32[]{:S(2)}) copy-start(f32[32,32,256]{2,1,0:T(8,128)} %copy-done.4) | copy-start | bytes 3145732
  165.9 21.5 %copy-start.1 = (f32[32,64,1,128]{3,2,1,0:T(1,128)S(1)}, f32[32,64,1,128]{3,2,1,0:T(1,128)}, u32[]{:S(2)}) copy-start(f32[32,64,1,128]{3,2,1,0:T(1,128)} %param.8) | copy-start | bytes 3145732
  179.3 33.5 %all-to-all-start.4 = ((f32[8,1,32768]{2,1,0:T(1,128)}), f32[8,1,32768]{2,1,0:T(1,128)}, u32[]{:S(2)}, u32[]{:S(2)}) async-start(f32[8,1,32768]{2,1,0:T(1,128)} %reshape.145), calls=%async_computation.4 | async-start | bytes 2097152 | tf_op jit(solution)/shard_map/all_to_all | solution.py:65
  217.1 6.5 %copy-start.3 = (f32[32,1,64,128]{3,2,1,0:T(8,128)S(1)}, f32[32,1,64,128]{3,2,1,0:T(8,128)}, u32[]{:S(2)}) copy-start(f32[32,1,64,128]{3,2,1,0:T(8,128)} %param.7) | copy-start | bytes 3145732
Sparse Core Ops, SparseCore 0:
  25.3 54.9 all-gather.1
where the time goes:
time: 233 us; the launch traced here: 232 us
  waiting for transfers between devices  69.7 us (30%)
  local copies, waits for them, and re-layouts  54.5 us (23%)
  starting transfers between devices  30.3 us (13%)
  matrix products  25.2 us (11%)
  between operations  18.2 us (8%)
  other arithmetic  17.4 us (7%)
  blocking collectives  16.6 us (7%)
    unnamed x19, local copies, waits for them, and re-layouts  22.3 us
    all_to_all x1, blocking collectives, from_everyone(): lax.all_to_all(jnp.broadcast_to(x[None], (peers, *x.shape)), axis, 0, 0,...  16.6 us
    all_gather x1, waiting for transfers between devices, body(): lax.all_gather(widened, 'row', axis=0, tiled=True)  16 us
    all_to_all x1, waiting for transfers between devices, body(): lax.all_to_all(flat_strip, 'row', split_axis=1, concat_axis=0, tiled=True)  14.1 us
    all_to_all x1, waiting for transfers between devices, body(): lax.all_to_all(strip_turned, 'col', split_axis=2, concat_axis=1, tiled=True)  13.5 us
    all_to_all x1, waiting for transfers between devices, body(): lax.all_to_all(z_turned, 'col', split_axis=2, concat_axis=1, tiled=True)  13.5 us
    all_to_all x1, waiting for transfers between devices, body(): lax.all_to_all(z_blocks, 'col', split_axis=1, concat_axis=2, tiled=True)  10.2 us
    all_to_all x1, starting transfers between devices, body(): lax.all_to_all(flat_strip, 'row', split_axis=1, concat_axis=0, tiled=True)  9.38 us
  transfers between devices with their start and end apart: 7, of which 6 were waited for; matrix products, arithmetic and copies ran while one was open for 34% of the time, Pallas kernels for 0%

commit v1 on v0

--- a/solution.py
+++ b/solution.py
@@ -4,6 +4,22 @@
 from jax.sharding import PartitionSpec as P
 
 W = 1024
+
+
+def pairwise_exchange(x, axis, split, join):
+    ways, here = (lax.axis_size(axis), lax.axis_index(axis))
+    width = x.shape[split] // ways
+    shape = list(x.shape)
+    shape[split] = width
+    height = shape[join]
+    shape[join] = height * ways
+    full = jnp.zeros(shape, x.dtype)
+    for mask in range(ways):
+        part = lax.dynamic_slice_in_dim(x, (here ^ mask) * width, width, axis=split)
+        if mask:
+            part = lax.ppermute(part, axis, [(d, d ^ mask) for d in range(ways)])
+        full = lax.dynamic_update_slice_in_dim(full, part, (here ^ mask) * height, axis=join)
+    return full
 
 
 def from_everyone(x, axis):
@@ -61,7 +77,7 @@
         rotation,
         precision=highest,
     )
-    z_rotated = lax.all_to_all(z_turned, "col", split_axis=2, concat_axis=1, tiled=True)
+    z_rotated = pairwise_exchange(z_turned, "col", 2, 1)
     strip_rotated = lax.all_to_all(strip_turned, "col", split_axis=2, concat_axis=1, tiled=True)
     row_count = lax.axis_size("row")
     round_number = jnp.arange(rounds, dtype=jnp.int32)[:, None]

time: 233 us -> 232 us (level)
  starting transfers between devices: 30.3 us -> 37.8 us
  waiting for transfers between devices: 69.7 us -> 66.3 us
    ppermute x0 -> x7, waiting for transfers between devices: none -> 22.6 us  [pairwise_exchange(): part = lax.ppermute(part, axis, [(d, d ^ mask) for d in range(ways)])]
    all_to_all x1, waiting for transfers between devices: 10.2 us -> 27.4 us  [body(): lax.all_to_all(z_blocks, 'col', split_axis=1, concat_axis=2, tiled=True)]
    all_gather x1, waiting for transfers between devices: 16 us -> 0.01 us  [body(): lax.all_gather(widened, 'row', axis=0, tiled=True)]
    all_to_all x1, waiting for transfers between devices: 14.1 us -> 0.01 us  [body(): lax.all_to_all(flat_strip, 'row', split_axis=1, concat_axis=0, tiled=True)]
    all_to_all x1, waiting for transfers between devices: 2.34 us -> 16.2 us  [body(): lax.all_to_all(strip_blocks, 'col', split_axis=1, concat_axis=2, tiled=True)]
    all_to_all x1, waiting for transfers between devices: 13.5 us -> 0.01 us  [body(): lax.all_to_all(strip_turned, 'col', split_axis=2, concat_axis=1, tiled=True)]
    all_to_all x1 -> x0, waiting for transfers between devices: 13.5 us -> none  [body(): lax.all_to_all(z_turned, 'col', split_axis=2, concat_axis=1, tiled=True)]
    ppermute x0 -> x7, starting transfers between devices: none -> 10.5 us  [pairwise_exchange(): part = lax.ppermute(part, axis, [(d, d ^ mask) for d in range(ways)])]
  transfers between devices with their start and end apart: 7 -> 13, of which waited for: 6 -> 3; matrix products, arithmetic and copies ran while one was open for 34% -> 29% of each run, Pallas kernels for 0% -> 0%
where the time goes in v1:
time: 232 us; the launch traced here: 231 us
  waiting for transfers between devices  66.3 us (29%)
  local copies, waits for them, and re-layouts  52.8 us (23%)
  starting transfers between devices  37.8 us (16%)
  matrix products  23.3 us (10%)
  between operations  18.4 us (8%)
  blocking collectives  16.6 us (7%)
  other arithmetic  15.5 us (7%)
    all_to_all x1, waiting for transfers between devices, body(): lax.all_to_all(z_blocks, 'col', split_axis=1, concat_axis=2, tiled=True)  27.4 us
    ppermute x7, waiting for transfers between devices, pairwise_exchange(): part = lax.ppermute(part, axis, [(d, d ^ mask) for d in range(ways)])  22.6 us
    all_to_all x1, blocking collectives, from_everyone(): lax.all_to_all(jnp.broadcast_to(x[None], (peers, *x.shape)), axis, 0, 0,...  16.6 us
    all_to_all x1, waiting for transfers between devices, body(): lax.all_to_all(strip_blocks, 'col', split_axis=1, concat_axis=2, tiled=True)  16.2 us
    unnamed x23, local copies, waits for them, and re-layouts  15.1 us
    ppermute x7, starting transfers between devices, pairwise_exchange(): part = lax.ppermute(part, axis, [(d, d ^ mask) for d in range(ways)])  10.5 us
    dynamic_update_slice x8, local copies, waits for them, and re-layouts, pairwise_exchange(): lax.dynamic_update_slice_in_dim(full, part, (here ^ mask) * height, axis=...  9.75 us
    all_to_all x1, starting transfers between devices, body(): lax.all_to_all(flat_strip, 'row', split_axis=1, concat_axis=0, tiled=True)  7.68 us
  transfers between devices with their start and end apart: 13, of which 3 were waited for; matrix products, arithmetic and copies ran while one was open for 29% of the time, Pallas kernels for 0%

profile of v1, /device:TPU:1, one launch (start us, length us, event | category | flops | bytes accessed | tf_op | source)
XLA Modules:
  0.0 230.7 jit_solution(10410297355325712757)
XLA Ops:
  8.0 16.6 %all_to_all.91 = f32[8,32,128]{2,1,0:T(8,128)S(1)} all-to-all(f32[8,32,128]{2,1,0:T(8,128)S(1)} %broadcast_in_dim.45), channel_id=1, replica_groups=mesh['row'=32,'col'=8] {'col'}, dimensions={0} | all-to-all | bytes 262144 | tf_op jit(solution)/shard_map/all_to_all | solution.py:27
  25.3 2.9 %copy.114 = f32[32,1,64,128]{3,0,2,1:T(8,128)} copy(f32[32,1,64,128]{3,2,1,0:T(8,128)} %param.6) | data formatting | bytes 2097152 | tf_op args[0]
  28.2 3.6 %all-to-all-start.1 = ((f32[32,64,128]{2,0,1:T(8,128)}), f32[32,64,128]{2,0,1:T(8,128)S(1)}, u32[]{:S(2)}, u32[]{:S(2)}) async-start(f32[32,64,128]{2,0,1:T(8,128)} %bitcast.104), calls=%async_computation.1 | async-start | bytes 2097152 | tf_op jit(solution)/shard_map/all_to_all | solution.py:70
  33.3 27.4 %all-to-all-done.1 = f32[32,64,128]{2,0,1:T(8,128)S(1)} async-done(((f32[32,64,128]{2,0,1:T(8,128)}), f32[32,64,128]{2,0,1:T(8,128)S(1)}, u32[]{:S(2)}, u32[]{:S(2)}) %all-to-all-start.1) | async-done | bytes 1048608 | tf_op jit(solution)/shard_map/all_to_all | solution.py:70
  61.7 3.6 %all-to-all-start.2 = ((f32[32,64,128]{2,0,1:T(8,128)}), f32[32,64,128]{2,0,1:T(8,128)S(1)}, u32[]{:S(2)}, u32[]{:S(2)}) async-start(f32[32,64,128]{2,0,1:T(8,128)} %bitcast.102), calls=%async_computation.2 | async-start | bytes 2097152 | tf_op jit(solution)/shard_map/all_to_all | solution.py:76
  67.2 3.2 %reduce.3 = f32[32,64,128]{2,1,0:T(8,128)S(1)} reduce(f32[32,64,1,128]{3,2,1,0:T(1,128)S(1)} %copy-done.1, f32[]{:T(128)} %broadcast.103), dimensions={2}, to_apply=%param.8.reduce_sub_computation.3 | reduce | bytes 2097156 | tf_op args[2]
  71.7 2.9 %copy.93 = f32[32,32,256]{2,0,1:T(8,128)} copy(f32[32,32,256]{2,1,0:T(8,128)} %all_to_all.79) | data formatting | bytes 2097152 | tf_op jit(solution)/shard_map/all_to_all | solution.py:92
  78.3 16.2 %all-to-all-done.2 = f32[32,64,128]{2,0,1:T(8,128)S(1)} async-done(((f32[32,64,128]{2,0,1:T(8,128)}), f32[32,64,128]{2,0,1:T(8,128)S(1)}, u32[]{:S(2)}, u32[]{:S(2)}) %all-to-all-start.2) | async-done | bytes 1048608 | tf_op jit(solution)/shard_map/all_to_all | solution.py:76
  94.5 7.7 %all-to-all-start.4 = ((f32[32,32,256]{2,0,1:T(8,128)}), f32[32,32,256]{2,0,1:T(8,128)}, u32[]{:S(2)}, u32[]{:S(2)}) async-start(f32[32,32,256]{2,0,1:T(8,128)} %copy.93), calls=%async_computation.4 | async-start | bytes 2097152 | tf_op jit(solution)/shard_map/all_to_all | solution.py:92
  107.9 5.6 %fusion.14 = f32[1,1024]{1,0:T(1,128)S(1)} fusion(f32[1024,1]{0,1:T(1,128)S(1)} %bitcast.116, f32[1024,1024]{1,0:T(8,128)} %all-gather.2.cloned.1.call-done), kind=kOutput, calls=%fused_computation.47 | convolution fusion | flops 12582912 | bytes 4202496 | tf_op jit(solution)/shard_map/dot_general | solution.py:52
  115.7 4.6 %fusion.4 = f32[1024,1024]{0,1:T(8,128)} fusion(f32[1024,1024]{1,0:T(8,128)} %all-gather.2.cloned.1.call-done, f32[1024]{0:T(1024)S(1)} %bitcast.112, f32[1024]{0:T(1024)S(1)} %broadcast_multiply_fusion), kind=kLoop, calls=%fused_computation.5 | loop fusion | flops 2097152 | bytes 8396800 | tf_op jit(solution)/shard_map/dot_general | solution.py:93
  120.3 5.4 %copy.92 = f32[1024,1024]{1,0:T(8,128)} copy(f32[1024,1024]{0,1:T(8,128)} %fusion.4) | data formatting | bytes 8388608 | tf_op jit(solution)/shard_map/dot_general | solution.py:93
  125.7 7.1 %fusion.15 = f32[32,32,256]{2,1,0:T(8,128)} fusion(f32[32,32,1024]{2,1,0:T(8,128)} %bitcast.98, f32[1024,256,1]{1,0,2:T(8,128)} %bitcast.40), kind=kOutput, calls=%fused_computation.48 | convolution fusion | flops 3221225472 | bytes 6291456 | tf_op jit(solution)/shard_map/dot_general | solution.py:93
  132.8 7.4 %all-to-all-start.5 = ((f32[32,32,256]{2,1,0:T(8,128)}), f32[32,32,256]{2,1,0:T(8,128)S(1)}, u32[]{:S(2)}, u32[]{:S(2)}) async-start(f32[32,32,256]{2,1,0:T(8,128)} %fusion.15), calls=%async_computation.5 | async-start | bytes 2097152 | tf_op jit(solution)/shard_map/all_to_all | solution.py:94
  140.2 6.3 %fusion.2 = f32[1024,32,8]{0,1,2:T(8,128)S(1)} fusion(f32[32,8,1024]{2,0,1:T(8,128)S(1)} %copy-done.6, f32[1024,1024]{1,0:T(8,128)} %all-gather.2.cloned.1.call-done, f32[1024]{0:T(1024)S(1)} %bitcast.113, f32[1024]{0:T(1024)S(1)} %broadcast_multiply_fusion), kind=kOutput, calls=%fused_computation.2 | convolution fusion | flops 3223322624 | bytes 6299648 | tf_op jit(solution)/shard_map/rbk,kj->rbj/dot_general | solution.py:68
  147.6 3.3 %collective-permute-start.2 = (f32[32,8,128]{2,0,1:T(8,128)}, f32[32,8,128]{2,0,1:T(8,128)}, u32[]{:S(2)}, u32[]{:S(2)}) collective-permute-start(f32[32,8,128]{2,0,1:T(8,128)} %get-tuple-element.19), channel_id=1, source_target_pairs={{0,3},{1,2},{2,1},{3,0},{4,7},{5,6},{6,5},{7,4},{8,11},{9,10},{10,... | collective-permute-start | bytes 393224 | tf_op jit(solution)/shard_map/ppermute | solution.py:20
  151.2 3.3 %collective-permute-start.4 = (f32[32,8,128]{2,0,1:T(8,128)}, f32[32,8,128]{2,0,1:T(8,128)}, u32[]{:S(2)}, u32[]{:S(2)}) collective-permute-start(f32[32,8,128]{2,0,1:T(8,128)} %get-tuple-element.17), channel_id=1, source_target_pairs={{0,5},{1,4},{2,7},{3,6},{4,1},{5,0},{6,3},{7,2},{8,13},{9,12},{10,... | collective-permute-start | bytes 393224 | tf_op jit(solution)/shard_map/ppermute | solution.py:20
  154.5 4.3 %fusion.9 = f32[32,8,1024]{2,0,1:T(8,128)S(1)} fusion(f32[32,8,1024]{2,0,1:T(8,128)S(1)} %copy-done.5, f32[1024,1024]{1,0:T(8,128)S(1)} %copy-done, f32[1024]{0:T(1024)S(1)} %bitcast.114, f32[1024]{0:T(1024)S(1)} %broadcast_multiply_fusion), kind=kOutput, calls=%fused_computation.10 | convolution fusion | flops 3223322624 | bytes 6299648 | tf_op jit(solution)/shard_map/rbk,kj->rbj/dot_general | solution.py:74
  161.5 4.8 %reshape.182 = f32[8,1,32768]{2,1,0:T(1,128)} reshape(f32[1024,8,32]{2,1,0:T(8,128)} %bitcast.96) | data formatting | bytes 2097152
  168.3 5.0 %all-to-all-start.3 = ((f32[8,1,32768]{2,1,0:T(1,128)}), f32[8,1,32768]{2,1,0:T(1,128)S(1)}, u32[]{:S(2)}, u32[]{:S(2)}) async-start(f32[8,1,32768]{2,1,0:T(1,128)} %reshape.182), calls=%async_computation.3 | async-start | bytes 2097152 | tf_op jit(solution)/shard_map/all_to_all | solution.py:81
  184.9 22.6 %collective-permute-done.6 = f32[32,8,128]{2,0,1:T(8,128)S(1)} collective-permute-done((f32[32,8,128]{2,0,1:T(8,128)S(1)}, f32[32,8,128]{2,0,1:T(8,128)S(1)}, u32[]{:S(2)}, u32[]{:S(2)}) %collective-permute-start.6) | collective-permute-done | bytes 131104 | tf_op jit(solution)/shard_map/ppermute | solution.py:20
  212.8 3.1 %reduce.4 = f32[8,32768]{1,0:T(8,128)S(1)} reduce(f32[8,1,32768]{2,1,0:T(1,128)S(1)} %all-to-all-done.3, f32[]{:T(128)} %broadcast.104), dimensions={1}, to_apply=%all_to_all.75.reduce_sub_computation | reduce | bytes 2097156 | tf_op jit(solution)/shard_map/all_to_all | solution.py:81
  215.9 3.3 %reshape.183 = f32[1024,8,32]{2,1,0:T(8,128)} reshape(f32[8,32768]{1,0:T(8,128)S(1)} %reduce.4) | data formatting | bytes 2097152
  219.3 3.2 %copy.91 = f32[32,8,8,128]{3,2,1,0:T(8,128)S(1)} copy(f32[32,8,8,128]{0,2,3,1:T(8,128)} %bitcast.97) | data formatting | bytes 2097152 | tf_op jit(solution)/shard_map/all_to_all | solution.py:81
  (70 shorter events, 38.9 us)
Async XLA Ops:
  7.2 24.6 %copy-start.2 = (f32[32,1,64,128]{3,2,1,0:T(8,128)S(1)}, f32[32,1,64,128]{3,2,1,0:T(8,128)}, u32[]{:S(2)}) copy-start(f32[32,1,64,128]{3,2,1,0:T(8,128)} %param.7) | copy-start | bytes 3145732
  7.2 96.7 %all-gather.2.cloned.1.call-start = ((), (), s32[]{:S(2)}) async-start(), calls=%async_computation.6 | async-start | bytes 4325376 | tf_op jit(solution)/shard_map/all_gather | solution.py:62
  25.3 41.9 %copy-start.1 = (f32[32,64,1,128]{3,2,1,0:T(1,128)S(1)}, f32[32,64,1,128]{3,2,1,0:T(1,128)}, u32[]{:S(2)}) copy-start(f32[32,64,1,128]{3,2,1,0:T(1,128)} %param.8) | copy-start | bytes 3145732
  28.2 32.6 %all-to-all-start.1 = ((f32[32,64,128]{2,0,1:T(8,128)}), f32[32,64,128]{2,0,1:T(8,128)S(1)}, u32[]{:S(2)}, u32[]{:S(2)}) async-start(f32[32,64,128]{2,0,1:T(8,128)} %bitcast.104), calls=%async_computation.1 | async-start | bytes 2097152 | tf_op jit(solution)/shard_map/all_to_all | solution.py:70
  60.8 1.0 copy-start.4
  61.7 32.7 %all-to-all-start.2 = ((f32[32,64,128]{2,0,1:T(8,128)}), f32[32,64,128]{2,0,1:T(8,128)S(1)}, u32[]{:S(2)}, u32[]{:S(2)}) async-start(f32[32,64,128]{2,0,1:T(8,128)} %bitcast.102), calls=%async_computation.2 | async-start | bytes 2097152 | tf_op jit(solution)/shard_map/all_to_all | solution.py:76
  94.5 31.2 %all-to-all-start.4 = ((f32[32,32,256]{2,0,1:T(8,128)}), f32[32,32,256]{2,0,1:T(8,128)}, u32[]{:S(2)}, u32[]{:S(2)}) async-start(f32[32,32,256]{2,0,1:T(8,128)} %copy.93), calls=%async_computation.4 | async-start | bytes 2097152 | tf_op jit(solution)/shard_map/all_to_all | solution.py:92
  125.7 14.5 %copy-start.6 = (f32[32,8,1024]{2,0,1:T(8,128)S(1)}, f32[32,8,1024]{2,0,1:T(8,128)}, u32[]{:S(2)}) copy-start(f32[32,8,1024]{2,0,1:T(8,128)} %all_to_all.70) | copy-start | bytes 3145732
  132.8 35.5 %all-to-all-start.5 = ((f32[32,32,256]{2,1,0:T(8,128)}), f32[32,32,256]{2,1,0:T(8,128)S(1)}, u32[]{:S(2)}, u32[]{:S(2)}) async-start(f32[32,32,256]{2,1,0:T(8,128)} %fusion.15), calls=%async_computation.5 | async-start | bytes 2097152 | tf_op jit(solution)/shard_map/all_to_all | solution.py:94
  140.2 14.3 %copy-start = (f32[1024,1024]{1,0:T(8,128)S(1)}, f32[1024,1024]{1,0:T(8,128)}, u32[]{:S(2)}) copy-start(f32[1024,1024]{1,0:T(8,128)} %all-gather.2.cloned.1.call-done) | copy-start | bytes 12582916
  140.2 14.3 %copy-start.5 = (f32[32,8,1024]{2,0,1:T(8,128)S(1)}, f32[32,8,1024]{2,0,1:T(8,128)}, u32[]{:S(2)}) copy-start(f32[32,8,1024]{2,0,1:T(8,128)} %all_to_all.74) | copy-start | bytes 3145732
  147.4 19.1 %collective-permute-start = (f32[32,8,128]{2,0,1:T(8,128)}, f32[32,8,128]{2,0,1:T(8,128)}, u32[]{:S(2)}, u32[]{:S(2)}) collective-permute-start(f32[32,8,128]{2,0,1:T(8,128)} %get-tuple-element.21), channel_id=1, source_target_pairs={{0,1},{1,0},{2,3},{3,2},{4,5},{5,4},{6,7},{7,6},{8,9},{9,8},{10,11... | collective-permute-start | bytes 393224 | tf_op jit(solution)/shard_map/ppermute | solution.py:20
  147.6 27.3 %collective-permute-start.1 = (f32[32,8,128]{2,0,1:T(8,128)}, f32[32,8,128]{2,0,1:T(8,128)}, u32[]{:S(2)}, u32[]{:S(2)}) collective-permute-start(f32[32,8,128]{2,0,1:T(8,128)} %get-tuple-element.20), channel_id=1, source_target_pairs={{0,2},{1,3},{2,0},{3,1},{4,6},{5,7},{6,4},{7,5},{8,10},{9,11},{10,... | collective-permute-start | bytes 393224 | tf_op jit(solution)/shard_map/ppermute | solution.py:20
  147.6 31.6 %collective-permute-start.2 = (f32[32,8,128]{2,0,1:T(8,128)}, f32[32,8,128]{2,0,1:T(8,128)}, u32[]{:S(2)}, u32[]{:S(2)}) collective-permute-start(f32[32,8,128]{2,0,1:T(8,128)} %get-tuple-element.19), channel_id=1, source_target_pairs={{0,3},{1,2},{2,1},{3,0},{4,7},{5,6},{6,5},{7,4},{8,11},{9,10},{10,... | collective-permute-start | bytes 393224 | tf_op jit(solution)/shard_map/ppermute | solution.py:20
  150.9 29.9 %collective-permute-start.3 = (f32[32,8,128]{2,0,1:T(8,128)}, f32[32,8,128]{2,0,1:T(8,128)}, u32[]{:S(2)}, u32[]{:S(2)}) collective-permute-start(f32[32,8,128]{2,0,1:T(8,128)} %get-tuple-element.18), channel_id=1, source_target_pairs={{0,4},{1,5},{2,6},{3,7},{4,0},{5,1},{6,2},{7,3},{8,12},{9,13},{10,... | collective-permute-start | bytes 393224 | tf_op jit(solution)/shard_map/ppermute | solution.py:20
  151.2 31.4 %collective-permute-start.4 = (f32[32,8,128]{2,0,1:T(8,128)}, f32[32,8,128]{2,0,1:T(8,128)}, u32[]{:S(2)}, u32[]{:S(2)}) collective-permute-start(f32[32,8,128]{2,0,1:T(8,128)} %get-tuple-element.17), channel_id=1, source_target_pairs={{0,5},{1,4},{2,7},{3,6},{4,1},{5,0},{6,3},{7,2},{8,13},{9,12},{10,... | collective-permute-start | bytes 393224 | tf_op jit(solution)/shard_map/ppermute | solution.py:20
  166.5 1.0 copy-start.7
  167.5 16.7 %collective-permute-start.5 = (f32[32,8,128]{2,0,1:T(8,128)S(1)}, f32[32,8,128]{2,0,1:T(8,128)S(1)}, u32[]{:S(2)}, u32[]{:S(2)}) collective-permute-start(f32[32,8,128]{2,0,1:T(8,128)S(1)} %get-tuple-element.16), channel_id=1, source_target_pairs={{0,6},{1,7},{2,4},{3,5},{4,2},{5,3},{6,0},{7,1},{8,14},{9,15},{10,... | collective-permute-start | bytes 393224 | tf_op jit(solution)/shard_map/ppermute | solution.py:20
  168.3 44.0 %all-to-all-start.3 = ((f32[8,1,32768]{2,1,0:T(1,128)}), f32[8,1,32768]{2,1,0:T(1,128)S(1)}, u32[]{:S(2)}, u32[]{:S(2)}) async-start(f32[8,1,32768]{2,1,0:T(1,128)} %reshape.182), calls=%async_computation.3 | async-start | bytes 2097152 | tf_op jit(solution)/shard_map/all_to_all | solution.py:81
  174.9 32.6 %collective-permute-start.6 = (f32[32,8,128]{2,0,1:T(8,128)S(1)}, f32[32,8,128]{2,0,1:T(8,128)S(1)}, u32[]{:S(2)}, u32[]{:S(2)}) collective-permute-start(f32[32,8,128]{2,0,1:T(8,128)S(1)} %get-tuple-element.15), channel_id=1, source_target_pairs={{0,7},{1,6},{2,5},{3,4},{4,3},{5,2},{6,1},{7,0},{8,15},{9,14},{10,... | collective-permute-start | bytes 393224 | tf_op jit(solution)/shard_map/ppermute | solution.py:20
  215.9 6.5 %copy-start.3 = (f32[32,1,64,128]{3,2,1,0:T(8,128)S(1)}, f32[32,1,64,128]{3,2,1,0:T(8,128)}, u32[]{:S(2)}) copy-start(f32[32,1,64,128]{3,2,1,0:T(8,128)} %param.7) | copy-start | bytes 3145732
  215.9 6.5 %copy-start.8 = (pred[32,64]{1,0:T(8,128)(4,1)S(1)}, pred[32,64]{1,0:T(8,128)(4,1)}, u32[]{:S(2)}) copy-start(pred[32,64]{1,0:T(8,128)(4,1)} %add_compare_fusion.1) | copy-start | bytes 6148
Sparse Core Ops, SparseCore 0:
  25.4 49.3 all-gather.1
